TPU v7x, 32 devices: a whole 2x2x4 slice. The times are simulated.
32 devices in a mesh: grp: 2 (over x), lon: 4 (over y, core), lat: 4 (over z).
Axes of the slice: x: 2, y: 2, z: 4, core: 2. Of those that a mesh axis runs over, the one named last changes fastest.
Arguments:
- fields: bfloat16 [6, 2, 48, 48, 512], P('grp', None, 'lat', 'lon'), may hold values from -6 to 6
- surface_mask: int32 [2, 48, 48], P(None, 'lat', 'lon'), may hold values 0 or 1
- w_qkv: bfloat16 [512, 1536], replicated, may hold values from -0.25 to 0.25
- w_out: bfloat16 [512, 512], replicated, may hold values from -0.25 to 0.25
- logit_scale: float32 [8], replicated, may hold values from 2 to 12
- mask_bias: float32 [8], replicated, may hold values from -2 to 2
- w_up: bfloat16 [512, 2048], replicated, may hold values from -0.25 to 0.25
- w_down: bfloat16 [2048, 512], replicated, may hold values from -0.125 to 0.125
Outputs:
- joined: bfloat16 [6, 2, 48, 48, 512], P('grp', None, 'lat', 'lon')
All inputs are finite; a program needn't handle non-finite values. No bound on the sum of `surface_mask` on one device may be relied on, other than what follows from the above.
Results may differ from a plain program's by a relative error of at most 0.006.
Values may be sent and summed in bfloat16 or wider, within the bound.
A program may use at most 128 MiB of HBM per device.

v0:
```python
import functools
import math

import jax
import jax.numpy as jnp
from jax import lax
from jax.experimental import pallas as pl
from jax.experimental.pallas import tpu as pltpu
from jax.sharding import PartitionSpec as P

SH_LAT = 3
SH_LON = 6
LOG2E = math.log2(math.e)
FAR = -30000.0
MESH = pl.DeviceIdType.MESH
BF16 = jnp.bfloat16
F32 = jnp.float32


def layer_norm(values):
    centred = values - jnp.mean(values, -1, keepdims=True)
    return centred * lax.rsqrt(jnp.mean(centred * centred, -1, keepdims=True) + 1e-05)


def iota(shape, axis):
    return lax.broadcasted_iota(jnp.int32, shape, axis)


def dot(left, right):
    return jnp.dot(left, right, preferred_element_type=F32)


def dot_t(left, right):
    return lax.dot_general(left, right, (((1,), (1,)), ((), ())), preferred_element_type=F32)


def kernel(
    real, heads,
    fields_hbm, mask_ref, scale_ref, bias_ref, wqkv_hbm, wout_hbm, wup_hbm, wdown_hbm,
    out_hbm,
    raw, tidy, x_ref, wqkv, wout, wup, wdown, win, ret, proj, att, qs, ks, vs, kx, acc, outs,
    wsem, osem, send1, recv1, send2, recv2,
):
    rows, width = x_ref.shape[2:]
    groups, nlat, lon_pairs, sub = raw.shape[:4]
    levels = mask_ref.shape[1]
    tiles = width // 128
    side_pairs = SH_LON // 2
    slab_rows = groups * SH_LAT * side_pairs * sub
    pair_rows = 2 * rows
    half = 2 * pair_rows
    total = 2 * half
    pairs = heads // 2
    head_size = width // heads
    lanes = 2 * head_size

    g, a, b = lax.axis_index("grp"), lax.axis_index("lat"), lax.axis_index("lon")
    na, nb = lax.axis_size("lat"), lax.axis_size("lon")

    barrier = pltpu.get_barrier_semaphore()
    greeted = 0
    for d in (0, 1):
        for da in (-1, 0, 1):
            for db in (-1, 0, 1):
                if d or da or db:
                    pl.semaphore_signal(
                        barrier,
                        inc=1,
                        device_id={
                            "grp": (g + d) % 2,
                            "lat": (a + da + na) % na,
                            "lon": (b + db + nb) % nb,
                        },
                        device_id_type=MESH,
                    )
                    greeted += 1
    load = pltpu.make_async_copy(fields_hbm, raw, wsem.at[4])
    load.start()
    weights = [
        pltpu.make_async_copy(src, dst, wsem.at[i])
        for i, (src, dst) in enumerate(
            ((wqkv_hbm, wqkv), (wout_hbm, wout), (wup_hbm, wup), (wdown_hbm, wdown))
        )
    ]
    for copy in weights:
        copy.start()

    def parity_to(d, cc):
        return (g + d + b + cc) % 2

    def row_of(parity, rr):
        return (1 + 2 * parity + rr) % 4

    def forward(r, d, act):
        parity, rr = (1, 1) if r == 0 else ((r - 1) // 2, (r - 1) % 2)
        cc = (parity + g + b + d) % 2
        p = 2 * d + cc
        src = x_ref.at[r, 1 - cc]
        dst = win.at[p, rr]
        i = 2 * p + rr

        def local():
            return pltpu.make_async_copy(src, dst, recv1.at[i])

        def remote():
            return pltpu.make_async_remote_copy(
                src_ref=src, dst_ref=dst, send_sem=send1.at[i], recv_sem=recv1.at[i],
                device_id={
                    "grp": (g + d) % 2,
                    "lat": (a - 1 + na) % na if r == 0 else a,
                    "lon": (b - cc + nb) % nb,
                },
                device_id_type=MESH,
            )

        if r == 0 or d:
            act(remote())
        else:
            pl.when(cc == 1)(lambda: act(remote()))
            if act is begin:
                pl.when(cc == 0)(lambda: act(local()))

    def begin(copy):
        copy.start()

    def drain(copy):
        copy.wait_send()

    def backward(d, cc, rr, act):
        parity = (g + b) % 2
        p = 2 * d + cc
        src = proj.at[p, rr]
        dst = ret.at[p, rr]
        i = 2 * p + rr
        edge = rr * parity

        def local():
            return pltpu.make_async_copy(src, dst, recv2.at[i])

        def remote():
            return pltpu.make_async_remote_copy(
                src_ref=src, dst_ref=dst, send_sem=send2.at[i], recv_sem=recv2.at[i],
                device_id={
                    "grp": (g + d) % 2,
                    "lat": (a + edge) % na,
                    "lon": (b + cc) % nb,
                },
                device_id_type=MESH,
            )

        act(d, cc, rr, parity, local, remote)

    def start(d, cc, rr, parity, local, remote):
        if d or cc:
            remote().start()
        elif rr == 0:
            local().start()
        else:
            pl.when(parity == 0)(lambda: local().start())
            pl.when(parity == 1)(lambda: remote().start())

    def finish(d, cc, rr, parity, local, remote):
        if d or cc:
            remote().wait_send()
        elif rr == 1:
            pl.when(parity == 1)(lambda: remote().wait_send())

    span_of = iota((tiles * rows, 1), 0)
    inside = span_of % rows
    place = jnp.where(
        inside < real,
        inside // levels * (tiles * levels) + span_of // rows * levels + inside % levels,
        -1,
    )
    pick = jnp.where(iota((tiles * rows, slab_rows), 1) == place, 1.0, 0.0).astype(BF16)

    tidy[...] = jnp.zeros_like(tidy)
    for i in range(nlat):
        tidy[levels * i : levels * (i + 1), : mask_ref.shape[2]] = mask_ref[i].astype(F32)
    spot = iota((8 * 128, 1), 0)
    block, inside = spot // 128, spot % 128
    cell = inside // levels
    at_lat = block // 2 * SH_LAT + cell // SH_LON % SH_LAT
    at_lat = at_lat * levels + inside % levels
    at_lon = block % 2 * SH_LON + cell % SH_LON
    at_lat = jnp.where(inside < real, at_lat, -1)
    by_lat = jnp.where(iota((8 * 128, tidy.shape[0]), 1) == at_lat, 1.0, 0.0).astype(BF16)
    by_cell = dot(by_lat, tidy[...].astype(BF16))
    by_cell = jnp.where(iota((8 * 128, 128), 1) == at_lon, by_cell, 0.0).astype(BF16)
    flags = dot_t(jnp.ones((16, 128), BF16), by_cell)
    flag_row = iota((16, 128), 0) == real - rows + 16

    with jax.named_scope("load"):
        load.wait()

    def sort_row(r):
        for c in (0, 1):
            piece = raw[:, SH_LAT * r : SH_LAT * (r + 1), side_pairs * c : side_pairs * (c + 1)]
            tall = dot(pick, piece.reshape(slab_rows, 128)).astype(BF16)
            for t in range(tiles):
                x_ref[r, c, :, 128 * t : 128 * (t + 1)] = tall[t * rows : (t + 1) * rows]
            k = 2 * r + c
            x_ref[r, c, rows - 16 :, :128] = jnp.where(
                flag_row,
                flags[:, 128 * k : 128 * (k + 1)],
                tall[rows - 16 : rows].astype(F32),
            ).astype(BF16)

    sort_row(0)
    with jax.named_scope("greet"):
        pl.semaphore_wait(barrier, greeted)
    for r in range(4):
        if r < 3:
            sort_row(r + 1)
        forward(r, 0, begin)
        if r > 1:
            forward(r - 1, 1, begin)
    forward(0, 1, begin)
    forward(3, 1, begin)

    last = jnp.where(a == na - 1, (g + b) % 2, 0)
    row_in_block = iota((pair_rows, lanes), 0) % rows
    valid = row_in_block < real
    lane = iota((pair_rows, lanes), 1)
    late = jnp.where(iota((pair_rows, lanes), 0) >= rows, last, 0)
    raw_bias = jnp.zeros((1, lanes), F32)
    qscale = jnp.zeros((1, width), F32)
    for h in range(heads):
        raw_bias = jnp.where(
            iota((1, lanes), 1) // 2 == h, bias_ref[h] * LOG2E, raw_bias
        )
        qscale = jnp.where(
            iota((1, width), 1) // head_size == h, scale_ref[h] * (LOG2E / head_size), qscale
        )
    bias_hi = raw_bias.astype(BF16).astype(F32)
    bias_row = jnp.where(iota(raw_bias.shape, 1) % 2 == 0, bias_hi, raw_bias - bias_hi)
    far = jnp.where(
        lane == 2 * heads, FAR * late.astype(F32),
        jnp.where(lane == 2 * heads + 1, FAR * (1 - late).astype(F32), 0.0),
    )
    span = 2 * lanes
    blocks = jnp.where(
        iota((span, span), 0) // head_size == iota((span, span), 1) // head_size,
        1.0 / head_size, 0.0,
    ).astype(BF16)
    eye = jnp.where(iota((rows, lanes), 0) == iota((rows, lanes), 1), 1.0, 0.0).astype(BF16)
    ones = jnp.where(valid, 1.0, 0.0).astype(BF16)

    with jax.named_scope("wait_w"):
        weights[0].wait()

    def project(p, carry):
        with jax.named_scope("wait_in"):
            for rr in (0, 1):
                pltpu.make_async_copy(win.at[p, rr], win.at[p, rr], recv1.at[2 * p + rr]).wait()
        both = win[p].reshape(pair_rows, width)
        normed = layer_norm(both.astype(F32)).astype(BF16)
        here = pl.ds(p * pair_rows, pair_rows)
        for part, store in ((0, qs), (1, ks)):
            for s in range(width // span):
                lo = s * span
                mixed = dot(normed, wqkv[:, part * width + lo : part * width + lo + span])
                square = dot((mixed * mixed).astype(BF16), blocks)
                unit = mixed * lax.rsqrt(square + 1e-06)
                if part == 0:
                    unit = unit * qscale[:, lo : lo + span]
                unit = unit.astype(BF16)
                store[2 * s, here] = unit[:, :lanes]
                store[2 * s + 1, here] = unit[:, lanes:]
        for s in range(width // span):
            lo = 2 * width + s * span
            mixed = dot(normed, wqkv[:, lo : lo + span])
            for k in (0, 1):
                vs[2 * s + k, here] = jnp.where(
                    valid, mixed[:, k * lanes : (k + 1) * lanes], 0.0
                ).astype(BF16)
        marks = jnp.concatenate(
            [
                dot_t(eye, jnp.broadcast_to(win[p, rr, real : real + 1, :lanes], (lanes, lanes)))
                for rr in (0, 1)
            ],
            0,
        )
        kx[here] = (marks * bias_row + far).astype(BF16)
        return carry

    def attend(q0, nq, k0, nk, first, final):
        q_lane = iota((nq, lanes), 1)
        q_late = jnp.where((iota((nq, lanes), 0) // rows) % 2 == 1, last, 0)
        q_region = jnp.where(
            q_lane == 2 * heads, (1 - q_late).astype(F32),
            jnp.where(q_lane == 2 * heads + 1, q_late.astype(F32), 0.0),
        )
        low = q_lane < head_size
        sides = [
            jnp.where(low if e == 0 else ~low, 1.0, 0.0).astype(BF16) for e in (0, 1)
        ]
        ones_all = jnp.concatenate([ones] * (nk // pair_rows), 0)

        def one_pair(pair, carry):
            query = qs[pair, q0 : q0 + nq]
            keys = jnp.concatenate([ks[pair, k0 : k0 + nk], kx[k0 : k0 + nk]], 1)
            values = jnp.concatenate([vs[pair, k0 : k0 + nk], ones_all], 1)
            asked = [
                jnp.concatenate(
                    [
                        query * sides[e],
                        jnp.where(q_lane // 2 == 2 * pair + e, 1.0, q_region).astype(BF16),
                    ],
                    1,
                )
                for e in (0, 1)
            ]
            if nq == pair_rows:
                summed = dot(jnp.exp2(dot_t(jnp.concatenate(asked, 0), keys)).astype(BF16), values)
                parts = [summed[:nq], summed[nq:]]
            else:
                parts = [dot(jnp.exp2(dot_t(ask, keys)).astype(BF16), values) for ask in asked]
            ratios = []
            for e in (0, 1):
                if not first:
                    parts[e] = parts[e] + acc[pair, e]
                if not final:
                    acc[pair, e] = parts[e]
                else:
                    ratios.append(parts[e][:, :lanes] / parts[e][:, lanes:])
            if final:
                att[:nq, pl.ds(pl.multiple_of(pair * lanes, lanes), lanes)] = jnp.where(
                    low, ratios[0], ratios[1]
                ).astype(BF16)
            return carry

        with jax.named_scope("attend"):
            lax.fori_loop(0, pairs, one_pair, 0)

    lax.fori_loop(0, 2, project, 0)
    attend(0, half, 0, half, True, False)
    lax.fori_loop(2, 4, project, 0)
    weights[1].wait()

    def far_queries(p):
        attend(p * pair_rows, pair_rows, 0, total, True, True)
        projected = dot(att[:pair_rows], wout[...]).astype(BF16)
        proj[p] = projected.reshape(2, rows, width)
        for rr in (1, 0):
            backward(1, p % 2, rr, start)

    far_queries(3)
    attend(0, half, half, half, False, True)
    projected = dot(att[...], wout[...]).astype(BF16)
    proj[:2] = projected.reshape(2, 2, rows, width)
    for cc in (1, 0):
        for rr in (1, 0):
            backward(0, cc, rr, start)
    far_queries(2)

    weights[2].wait()
    weights[3].wait()

    def join(step, carry):
        p = jnp.where(step < 2, step, 5 - step)
        with jax.named_scope("wait_back"):
            for rr in (0, 1):
                pltpu.make_async_copy(ret.at[p, rr], ret.at[p, rr], recv2.at[2 * p + rr]).wait()
        d, cc = p // 2, p % 2
        parity = parity_to(d, cc)
        r0, r1 = row_of(parity, 0), row_of(parity, 1)
        own = jnp.concatenate([x_ref[r0, 1 - cc], x_ref[r1, 1 - cc]], 0)
        back = ret[p].reshape(pair_rows, width)
        residual = (own.astype(F32) + back.astype(F32)).astype(BF16).astype(F32)
        mlp_in = layer_norm(residual).astype(BF16)
        update = jnp.zeros_like(residual)
        hidden_size = wup.shape[1]
        piece = 512
        for s in range(hidden_size // piece):
            up = dot(mlp_in, wup[:, s * piece : (s + 1) * piece])
            slope = math.sqrt(2.0 / math.pi)
            bent = jnp.tanh(up * (slope + 0.044715 * slope * (up * up)))
            twice = (up + up * bent).astype(BF16)
            update = update + dot(twice, wdown[s * piece : (s + 1) * piece, :])
        joined = (residual + 0.5 * update).astype(BF16)
        for k, r in enumerate((r0, r1)):
            own_rows = joined[k * rows : (k + 1) * rows]
            tall = jnp.concatenate(
                [own_rows[:, 128 * t : 128 * (t + 1)] for t in range(tiles)], 0
            )
            i = 2 * p + k
            outs[i] = dot(put, tall).astype(BF16).reshape(outs.shape[1:])
            deliver(r, 1 - cc, i).start()
        return carry

    def deliver(r, c, i):
        rim = pl.ds(SH_LAT * r, SH_LAT)
        return pltpu.make_async_copy(
            outs.at[i], out_hbm.at[:, rim, pl.ds(side_pairs * c, side_pairs)], osem.at[i]
        )

    span_of = iota((1, tiles * rows), 1)
    inside = span_of % rows
    place = jnp.where(
        inside < real,
        inside // levels * (tiles * levels) + span_of // rows * levels + inside % levels,
        -1,
    )
    put = jnp.where(iota((slab_rows, tiles * rows), 0) == place, 1.0, 0.0).astype(BF16)

    lax.fori_loop(0, 4, join, 0)

    with jax.named_scope("drain"):
        for d in (0, 1):
            for r in range(4):
                forward(r, d, drain)
        for d in (0, 1):
            for cc in (0, 1):
                for rr in (0, 1):
                    backward(d, cc, rr, finish)
        for p in range(4):
            for k in (0, 1):
                r = row_of(parity_to(p // 2, p % 2), k)
                deliver(r, 1 - p % 2, 2 * p + k).wait()


def hand_over(src, dst, held, in_sem, out_sem):
    takes = [pltpu.make_async_copy(src.at[i], held.at[i], in_sem.at[i]) for i in range(src.shape[0])]
    gives = [pltpu.make_async_copy(held.at[i], dst.at[i], out_sem.at[i]) for i in range(src.shape[0])]
    for take in takes:
        take.start()
    for take, give in zip(takes, gives):
        take.wait()
        give.start()
    for give in gives:
        give.wait()


def per_device(fields, surface_mask, w_qkv, w_out, logit_scale, mask_bias, w_up, w_down):
    groups, levels, nlat, nlon, width = fields.shape
    heads = logit_scale.shape[0]
    head_size = width // heads
    hidden_size = w_up.shape[1]
    tris, sides = nlat // SH_LAT, nlon // SH_LON
    real = groups * levels * SH_LAT * SH_LON
    rows = -(-(real + 1) // 16) * 16
    total = 8 * rows

    tiles = width // 128
    raw = fields.reshape(groups, levels, nlat, nlon, tiles, 128)
    raw = jnp.transpose(raw, (0, 2, 3, 4, 1, 5))
    raw = raw.reshape(groups, nlat, nlon // 2, 2 * tiles * levels, 128)

    vmem = pl.BlockSpec(memory_space=pltpu.VMEM)
    scalars = pl.BlockSpec(memory_space=pltpu.SMEM)
    anywhere = pl.BlockSpec(memory_space=pl.ANY)
    joined = pl.pallas_call(
        functools.partial(kernel, real, heads),
        out_shape=jax.ShapeDtypeStruct(raw.shape, BF16),
        in_specs=[anywhere, vmem, scalars, scalars] + [anywhere] * 4,
        out_specs=anywhere,
        scratch_shapes=[
            pltpu.VMEM(raw.shape, BF16),
            pltpu.VMEM((nlat * levels, 128), F32),
            pltpu.VMEM((tris, sides, rows, width), BF16),
            pltpu.VMEM(w_qkv.shape, BF16),
            pltpu.VMEM(w_out.shape, BF16),
            pltpu.VMEM(w_up.shape, BF16),
            pltpu.VMEM(w_down.shape, BF16),
            pltpu.VMEM((4, 2, rows, width), BF16),
            pltpu.VMEM((4, 2, rows, width), BF16),
            pltpu.VMEM((4, 2, rows, width), BF16),
            pltpu.VMEM((total // 2, width), BF16),
            pltpu.VMEM((heads // 2, total, 2 * head_size), BF16),
            pltpu.VMEM((heads // 2, total, 2 * head_size), BF16),
            pltpu.VMEM((heads // 2, total, 2 * head_size), BF16),
            pltpu.VMEM((total, 2 * head_size), BF16),
            pltpu.VMEM((heads // 2, 2, total // 2, 4 * head_size), F32),
            pltpu.VMEM((8, groups, SH_LAT, SH_LON // 2) + raw.shape[3:], BF16),
            pltpu.SemaphoreType.DMA((5,)),
            pltpu.SemaphoreType.DMA((8,)),
            pltpu.SemaphoreType.DMA((8,)),
            pltpu.SemaphoreType.DMA((8,)),
            pltpu.SemaphoreType.DMA((8,)),
            pltpu.SemaphoreType.DMA((8,)),
        ],
        compiler_params=pltpu.CompilerParams(
            collective_id=0, has_side_effects=True, vmem_limit_bytes=56 * 1024 * 1024
        ),
        name="window_block",
    )(raw, jnp.transpose(surface_mask, (1, 0, 2)), logit_scale, mask_bias, w_qkv, w_out, w_up, w_down)

    joined = pl.pallas_call(
        hand_over,
        out_shape=jax.ShapeDtypeStruct(raw.shape, BF16),
        in_specs=[anywhere],
        out_specs=anywhere,
        scratch_shapes=[
            pltpu.VMEM(raw.shape, BF16),
            pltpu.SemaphoreType.DMA((groups,)),
            pltpu.SemaphoreType.DMA((groups,)),
        ],
        name="hand_over",
    )(joined)
    joined = joined.reshape(groups, nlat, nlon, tiles, levels, 128)
    return jnp.transpose(joined, (0, 4, 1, 2, 3, 5)).reshape(fields.shape)


def solution(mesh):
    return jax.shard_map(
        per_device,
        mesh=mesh,
        in_specs=(
            P("grp", None, "lat", "lon", None),
            P(None, "lat", "lon"),
            P(),
            P(),
            P(),
            P(),
            P(),
            P(),
        ),
        out_specs=P("grp", None, "lat", "lon", None),
        check_vma=False,
    )
```

profile of v0, /device:TPU:1, one launch (start us, length us, event | category | flops | bytes accessed | tf_op | source)
XLA Modules:
  0.0 44.6 jit_solution(18258024978908458650)
XLA Ops:
  0.0 42.7 %window_block.1.src = bf16[3,12,6,16,128]{4,3,2,1,0:T(8,128)(2,1)} custom-call(bf16[3,12,6,16,128]{4,3,2,1,0:T(8,128)(2,1)} %bitcast.11, s32[12,2,12]{2,1,0:T(2,128)} %bitcast.12, f32[8]{0:T(128)} %scale_ref.1, f32[8]{0:T(128)} %bias_ref.1, bf16[512,1536]{1,0:T(8,128)(2,1)} %wqkv_hbm.1, bf16[512,512]{1,0:T(8,128)(2,1)} %wout_hbm.1, ...), custom_call_target="tpu_custom_call" | custom-call | tf_op jit(solution)/shard_map/window_block/pallas_call | solution.py:453
  42.7 1.9 %hand_over.1 = bf16[3,12,6,16,128]{4,3,2,1,0:T(8,128)(2,1)} custom-call(bf16[3,12,6,16,128]{4,3,2,1,0:T(8,128)(2,1)} %window_block.1.src), custom_call_target="tpu_custom_call" | custom-call | tf_op jit(solution)/shard_map/hand_over/pallas_call | solution.py:489
where the time goes:
time: 44.8 us; the launch traced here: 44.6 us
  Pallas kernels  44.6 us (100%)
    pallas_call x1, Pallas kernels, per_device(): pl.pallas_call(functools.partial(kernel, real, heads), out_shape=jax.Shap...  42.7 us
    pallas_call x1, Pallas kernels, per_device(): pl.pallas_call(hand_over, out_shape=jax.ShapeDtypeStruct(raw.shape, BF16)...  1.92 us

commit v1 on v0

v1 whole, which is shorter than its diff:
```python
import functools
import math

import jax
import jax.numpy as jnp
from jax import lax
from jax.experimental import pallas as pl
from jax.experimental.pallas import tpu as pltpu
from jax.sharding import PartitionSpec as P

SH_LAT = 3
SH_LON = 6
LOG2E = math.log2(math.e)
FAR = -30000.0
MESH = pl.DeviceIdType.MESH
BF16 = jnp.bfloat16
F32 = jnp.float32


def layer_norm(values):
    centred = values - jnp.mean(values, -1, keepdims=True)
    return centred * lax.rsqrt(jnp.mean(centred * centred, -1, keepdims=True) + 1e-05)


def iota(shape, axis):
    return lax.broadcasted_iota(jnp.int32, shape, axis)


def dot(left, right):
    return jnp.dot(left, right, preferred_element_type=F32)


def dot_t(left, right):
    return lax.dot_general(left, right, (((1,), (1,)), ((), ())), preferred_element_type=F32)


def kernel(
    real, heads,
    fields_hbm, mask_hbm, scale_hbm, bias_hbm, wqkv_hbm, wout_hbm, wup_hbm, wdown_hbm,
    out_ref,
    raw, mask_ref, scale_ref, bias_ref, tidy, marked, rin, win, wqkv, wout, wup, wdown, att, qs, ks, vs,
    kx, acc, rout, sort0, sort1, put0, put1, blocks, soft,
    wsem, ssem, msend, mrecv, send1, recv1, send2, recv2,
):
    rows, width = win.shape[2:]
    levels = mask_ref.shape[1]
    nlat = mask_ref.shape[0]
    tiles = width // 128
    side_pairs = SH_LON // 2
    slab = rin.shape[1:]
    slab_rows = slab[0] * slab[1] * slab[2] * slab[3]
    pair_rows = 2 * rows
    half = 2 * pair_rows
    total = 2 * half
    pairs = heads // 2
    head_size = width // heads
    lanes = 2 * head_size
    cut_rows = 256
    cut = cut_rows // tiles

    g, a, b = lax.axis_index("grp"), lax.axis_index("lat"), lax.axis_index("lon")
    na, nb = lax.axis_size("lat"), lax.axis_size("lon")
    mine = (g + b) % 2

    def peer(d, da, db):
        return {"grp": (g + d) % 2, "lat": (a + da + na) % na, "lon": (b + db + nb) % nb}

    barrier = pltpu.get_barrier_semaphore()
    greeted = 0
    for d in (0, 1):
        for da, db in ((0, 0), (-1, 0), (0, -1), (-1, -1), (1, 0), (0, 1), (1, 1)):
            if d or da or db:
                pl.semaphore_signal(barrier, inc=1, device_id=peer(d, da, db), device_id_type=MESH)
                greeted += 1

    def row_of(parity, rr):
        return (1 + 2 * parity + rr) % 4

    def block_of(ref, parity, cc, rr):
        r = row_of(parity, rr)
        return ref.at[:, pl.ds(SH_LAT * r, SH_LAT), pl.ds(side_pairs * (1 - cc), side_pairs)]

    def by_owner(d, cc, rr, local, remote):
        if d or cc:
            remote()
        elif rr == 0:
            if local is not None:
                local()
        else:
            pl.when(mine == 1)(remote)
            if local is not None:
                pl.when(mine == 0)(local)

    def stay(cc, rr):
        i = 2 * rr + cc
        return pltpu.make_async_copy(block_of(fields_hbm, mine, cc, rr), rin.at[i], recv1.at[i])

    def forward(d, cc, rr):
        i = 4 * d + 2 * rr + cc
        parity = (g + b + d + cc) % 2
        return pltpu.make_async_remote_copy(
            src_ref=block_of(raw, parity, cc, rr), dst_ref=rin.at[i],
            send_sem=send1.at[i], recv_sem=recv1.at[i],
            device_id=peer(d, -rr * parity, -cc), device_id_type=MESH,
        )

    def backward(d, cc, rr):
        i = 4 * d + 2 * rr + cc
        return pltpu.make_async_remote_copy(
            src_ref=rout.at[i], dst_ref=block_of(out_ref, mine, cc, rr),
            send_sem=send2.at[i], recv_sem=recv2.at[i],
            device_id=peer(d, rr * mine, cc), device_id_type=MESH,
        )

    def settle(cc, rr):
        i = 2 * rr + cc
        return pltpu.make_async_copy(rout.at[i], block_of(out_ref, mine, cc, rr), recv2.at[i])

    def share(n):
        da, db = ((0, -1), (-1, 0), (-1, -1))[n]
        return pltpu.make_async_remote_copy(
            src_ref=tidy, dst_ref=marked.at[n], send_sem=msend.at[n], recv_sem=mrecv.at[n],
            device_id=peer(0, da, db), device_id_type=MESH,
        )

    load = pltpu.make_async_copy(fields_hbm, raw, wsem.at[4])
    load.start()
    small = [
        pltpu.make_async_copy(src, dst, ssem.at[i])
        for i, (src, dst) in enumerate(
            ((mask_hbm, mask_ref), (scale_hbm, scale_ref), (bias_hbm, bias_ref))
        )
    ]
    for copy in small:
        copy.start()
    stay(0, 0).start()
    pl.when(mine == 0)(lambda: stay(0, 1).start())
    weights = [
        pltpu.make_async_copy(src, dst, wsem.at[i])
        for i, (src, dst) in enumerate(
            ((wqkv_hbm, wqkv), (wout_hbm, wout), (wup_hbm, wup), (wdown_hbm, wdown))
        )
    ]
    for copy in weights:
        copy.start()

    for copy in small:
        copy.wait()
    tidy[...] = jnp.zeros_like(tidy)
    for i in range(nlat):
        tidy[levels * i : levels * (i + 1), : mask_ref.shape[2]] = mask_ref[i].astype(F32)

    load.wait()
    pl.semaphore_wait(barrier, greeted)
    order = [(d, cc, rr) for rr in (0, 1) for cc in (0, 1) for d in (1, 0)]
    for d, cc, rr in order:
        by_owner(d, cc, rr, None, lambda: forward(d, cc, rr).start())
    for n in range(3):
        share(n).start()

    def shuffle(count, held, out_rows, raw_out):
        shape = (out_rows, held * tiles) if raw_out else (held * tiles, out_rows)
        tall, flat = iota(shape, 1 if raw_out else 0), iota(shape, 0 if raw_out else 1)
        token, tile = tall % held, tall // held
        place = token // levels * (tiles * levels) + tile * levels + token % levels
        return jnp.where((place == flat) & (token < count), 1.0, 0.0).astype(BF16)

    rest = real - cut
    rest_held = rows - cut
    cuts = ((0, cut, cut, cut_rows), (cut, rest, rest_held, slab_rows - cut_rows))
    sorts, puts = (sort0, sort1), (put0, put1)
    for (_, count, held, n), pick, put in zip(cuts, sorts, puts):
        pick[...] = shuffle(count, held, n, False)
        put[...] = shuffle(count, held, n, True)

    last = jnp.where(a == na - 1, mine, 0)
    row_in_block = iota((pair_rows, lanes), 0) % rows
    valid = row_in_block < real
    raw_bias = jnp.zeros((1, lanes), F32)
    qscale = jnp.zeros((1, width), F32)
    for h in range(heads):
        raw_bias = jnp.where(
            iota((1, lanes), 1) // 2 == h, bias_ref[h] * LOG2E, raw_bias
        )
        qscale = jnp.where(
            iota((1, width), 1) // head_size == h, scale_ref[h] * (LOG2E / head_size), qscale
        )
    bias_hi = raw_bias.astype(BF16).astype(F32)
    bias_row = jnp.where(iota(raw_bias.shape, 1) % 2 == 0, bias_hi, raw_bias - bias_hi)
    span = 2 * lanes
    blocks[...] = jnp.where(
        iota((span, span), 0) // head_size == iota((span, span), 1) // head_size,
        1.0 / head_size, 0.0,
    ).astype(BF16)
    ones = jnp.where(valid, 1.0, 0.0).astype(BF16)

    def arrive(p):
        for cc in (0, 1):
            i = 2 * p + cc
            pltpu.make_async_copy(rin.at[i], rin.at[i], recv1.at[i]).wait()
        both = jnp.concatenate([rin[2 * p + cc].reshape(slab_rows, 128) for cc in (0, 1)], 1)
        start = 0
        for (token, _, held, n), pick in zip(cuts, sorts):
            tall = dot(pick[...], both[start : start + n]).astype(BF16)
            start += n
            for cc in (0, 1):
                for t in range(tiles):
                    win[p, cc, token : token + held, 128 * t : 128 * (t + 1)] = tall[
                        t * held : (t + 1) * held, 128 * cc : 128 * (cc + 1)
                    ]

    def mark(rr, carry):
        token = iota((rows, 1), 0)
        cell = token // levels
        lane = iota((rows, lanes), 1)
        late = (rr * last).astype(F32)
        far = jnp.where(
            lane == 2 * heads, FAR * late, jnp.where(lane == 2 * heads + 1, FAR * (1 - late), 0.0)
        )
        over = (rr * mine).astype(F32)
        for cc in (0, 1):
            near = tidy[...] if cc == 0 else marked[0]
            near = near + over * (marked[1 + cc] - near)
            at_lat = (SH_LAT * row_of(mine, rr) + cell // SH_LON % SH_LAT) * levels + token % levels
            at_lon = (1 - cc) * SH_LON + cell % SH_LON
            by_lat = jnp.where(iota((rows, tidy.shape[0]), 1) == at_lat, 1.0, 0.0).astype(BF16)
            by_cell = dot(by_lat, near.astype(BF16))
            by_cell = jnp.where(iota((rows, 128), 1) == at_lon, by_cell, 0.0).astype(BF16)
            marks = dot(by_cell, jnp.ones((128, lanes), BF16))
            key = (marks * bias_row + far).astype(BF16)
            for d in (0, 1):
                at = pl.multiple_of((2 * d + rr) * pair_rows + cc * rows, 16)
                kx[pl.ds(at, rows)] = key
        return carry

    def project(p):
        both = win[p].reshape(pair_rows, width)
        normed = layer_norm(both.astype(F32)).astype(BF16)
        here = pl.ds(pl.multiple_of(p * pair_rows, 16), pair_rows)
        spans = width // span

        def mix(part, s):
            lo = part * width + s * span
            return dot(normed, wqkv[:, lo : lo + span])

        def unify(part, s, mixed):
            square = dot((mixed * mixed).astype(BF16), blocks[...])
            unit = mixed * lax.rsqrt(square + 1e-06)
            if part == 0:
                unit = unit * qscale[:, s * span : (s + 1) * span]
            unit = unit.astype(BF16)
            store = ks if part else qs
            store[2 * s, here] = unit[:, :lanes]
            store[2 * s + 1, here] = unit[:, lanes:]

        def keep(s, mixed):
            for k in (0, 1):
                vs[2 * s + k, here] = jnp.where(
                    valid, mixed[:, k * lanes : (k + 1) * lanes], 0.0
                ).astype(BF16)

        jobs = [(part, s) for part in (0, 1) for s in range(spans)]
        waiting = []
        for part, s in jobs:
            waiting.append((part, s, mix(part, s)))
            if len(waiting) > 1:
                unify(*waiting.pop(0))
        for s in range(spans):
            mixed = mix(2, s)
            if waiting:
                unify(*waiting.pop(0))
            keep(s, mixed)

    q_lane = iota((pair_rows, lanes), 1)
    low = q_lane < head_size
    sides = [jnp.where(low if e == 0 else ~low, 1.0, 0.0).astype(BF16) for e in (0, 1)]
    ones_all = jnp.concatenate([ones, ones], 0)

    def attend(q, k0, sink):
        here = pl.ds(pl.multiple_of(q * pair_rows, 16), pair_rows)
        q_late = (q % 2 * last).astype(F32)
        q_region = jnp.where(
            q_lane == 2 * heads, 1 - q_late, jnp.where(q_lane == 2 * heads + 1, q_late, 0.0)
        )

        def weigh(pair):
            query = qs[pair, here]
            keys = jnp.concatenate([ks[pair, k0 : k0 + half], kx[k0 : k0 + half]], 1)
            asked = [
                jnp.concatenate(
                    [
                        query * sides[e],
                        jnp.where(q_lane // 2 == 2 * pair + e, 1.0, q_region).astype(BF16),
                    ],
                    1,
                )
                for e in (0, 1)
            ]
            soft[pair % 2] = jnp.exp2(dot_t(jnp.concatenate(asked, 0), keys)).astype(BF16)

        def gain(pair):
            values = jnp.concatenate([vs[pair, k0 : k0 + half], ones_all], 1)
            summed = dot(soft[pair % 2], values)
            up, down = summed[:pair_rows], summed[pair_rows:]
            sink(
                pair,
                jnp.where(low, up[:, :lanes], down[:, :lanes]),
                jnp.where(low, up[:, lanes:], down[:, lanes:]),
            )

        weigh(0)
        for pair in range(pairs):
            if pair + 1 < pairs:
                weigh(pair + 1)
            gain(pair)

    def attend_near(q, carry):
        def sink(pair, above, below):
            acc[q, pair, 0] = above
            acc[q, pair, 1] = below

        attend(q, 0, sink)
        return carry

    def attend_far(q):
        def sink(pair, above, below):
            ratio = (above + acc[q, pair, 0]) / (below + acc[q, pair, 1])
            att[:, pair * lanes : (pair + 1) * lanes] = ratio.astype(BF16)

        attend(q, half, sink)

    def join(p):
        projected = dot(att[...], wout[...]).astype(BF16)
        own = win[p].reshape(pair_rows, width)
        residual = (own.astype(F32) + projected.astype(F32)).astype(BF16).astype(F32)
        mlp_in = layer_norm(residual).astype(BF16)
        update = jnp.zeros_like(residual)
        hidden_size = wup.shape[1]
        piece = 512
        slope = math.sqrt(2.0 / math.pi)

        def raise_(s):
            up = dot(mlp_in, wup[:, s * piece : (s + 1) * piece])
            bent = jnp.tanh(up * (slope + 0.044715 * slope * (up * up)))
            return (up + up * bent).astype(BF16)

        pieces = hidden_size // piece
        twice = raise_(0)
        for s in range(pieces):
            later = raise_(s + 1) if s + 1 < pieces else None
            update = update + dot(twice, wdown[s * piece : (s + 1) * piece, :])
            twice = later
        joined = (residual + 0.5 * update).astype(BF16)
        flat = []
        for (token, _, held, _), put in zip(cuts, puts):
            tall = jnp.concatenate(
                [
                    jnp.concatenate(
                        [
                            joined[cc * rows + token : cc * rows + token + held, 128 * t : 128 * (t + 1)]
                            for t in range(tiles)
                        ],
                        0,
                    )
                    for cc in (0, 1)
                ],
                1,
            )
            flat.append(dot(put[...], tall).astype(BF16))
        flat = jnp.concatenate(flat, 0)
        d, rr = p // 2, p % 2
        for cc in (1, 0):
            rout[2 * p + cc] = flat[:, 128 * cc : 128 * (cc + 1)].reshape(slab)
            if cc == 1:
                backward(d, cc, rr).start()
            else:
                away = d + rr * mine
                pl.when(away > 0)(lambda: backward(d, 0, rr).start())
                pl.when(away == 0)(lambda: settle(0, rr).start())

    weights[0].wait()

    def gather(t, carry):
        arrive(t)
        project(t)
        first = jnp.where(t == 1, 0, t)
        lax.fori_loop(first, jnp.where(t == 0, 0, t + 1), attend_near, 0)
        return carry

    def scatter(t, carry):
        p = 3 - t
        attend_far(p)
        join(p)
        return carry

    for n in range(3):
        pltpu.make_async_copy(marked.at[n], marked.at[n], mrecv.at[n]).wait()
    lax.fori_loop(0, 2, mark, 0)
    lax.fori_loop(0, 4, gather, 0)
    for copy in weights[1:]:
        copy.wait()
    lax.fori_loop(0, 4, scatter, 0)

    for n in range(3):
        share(n).wait_send()
    for d, cc, rr in order:
        by_owner(d, cc, rr, None, lambda: forward(d, cc, rr).wait_send())
    for d, cc, rr in order:
        by_owner(d, cc, rr, None, lambda: backward(d, cc, rr).wait_send())
    for d, cc, rr in order:
        landed = block_of(out_ref, (g + b + d + cc) % 2, cc, rr)
        pltpu.make_async_copy(landed, landed, recv2.at[4 * d + 2 * rr + cc]).wait()


def hand_over(src, dst, sem):
    gives = [pltpu.make_async_copy(src.at[i], dst.at[i], sem.at[i]) for i in range(src.shape[0])]
    for give in gives:
        give.start()
    for give in gives:
        give.wait()


def per_device(fields, surface_mask, w_qkv, w_out, logit_scale, mask_bias, w_up, w_down):
    groups, levels, nlat, nlon, width = fields.shape
    heads = logit_scale.shape[0]
    head_size = width // heads
    real = groups * levels * SH_LAT * SH_LON
    rows = -(-real // 16) * 16
    total = 8 * rows

    tiles = width // 128
    raw = fields.reshape(groups, levels, nlat, nlon, tiles, 128)
    raw = jnp.transpose(raw, (0, 2, 3, 4, 1, 5))
    raw = raw.reshape(groups, nlat, nlon // 2, 2 * tiles * levels, 128)
    slab = (groups, SH_LAT, SH_LON // 2) + raw.shape[3:]

    cut = 256 // tiles
    spans = ((256, cut * tiles), (math.prod(slab[:-1]) - 256, (rows - cut) * tiles))
    orders = [(held, flat) for flat, held in spans] + list(spans)

    vmem = pl.BlockSpec(memory_space=pltpu.VMEM)
    anywhere = pl.BlockSpec(memory_space=pl.ANY)
    joined = pl.pallas_call(
        functools.partial(kernel, real, heads),
        out_shape=pltpu.VMEM(raw.shape, BF16),
        in_specs=[anywhere] * 8,
        out_specs=anywhere,
        scratch_shapes=[
            pltpu.VMEM(raw.shape, BF16),
            pltpu.VMEM((nlat, levels, nlon), jnp.int32),
            pltpu.SMEM(logit_scale.shape, F32),
            pltpu.SMEM(mask_bias.shape, F32),
            pltpu.VMEM((nlat * levels, 128), F32),
            pltpu.VMEM((3, nlat * levels, 128), F32),
            pltpu.VMEM((8,) + slab, BF16),
            pltpu.VMEM((4, 2, rows, width), BF16),
            pltpu.VMEM(w_qkv.shape, BF16),
            pltpu.VMEM(w_out.shape, BF16),
            pltpu.VMEM(w_up.shape, BF16),
            pltpu.VMEM(w_down.shape, BF16),
            pltpu.VMEM((total // 4, width), BF16),
            pltpu.VMEM((heads // 2, total, 2 * head_size), BF16),
            pltpu.VMEM((heads // 2, total, 2 * head_size), BF16),
            pltpu.VMEM((heads // 2, total, 2 * head_size), BF16),
            pltpu.VMEM((total, 2 * head_size), BF16),
            pltpu.VMEM((4, heads // 2, 2, total // 4, 2 * head_size), F32),
            pltpu.VMEM((8,) + slab, BF16),
        ]
        + [pltpu.VMEM(shape, BF16) for shape in orders]
        + [
            pltpu.VMEM((4 * head_size, 4 * head_size), BF16),
            pltpu.VMEM((2, total // 2, total // 2), BF16),
            pltpu.SemaphoreType.DMA((5,)),
            pltpu.SemaphoreType.DMA((3,)),
            pltpu.SemaphoreType.DMA((3,)),
            pltpu.SemaphoreType.DMA((3,)),
            pltpu.SemaphoreType.DMA((8,)),
            pltpu.SemaphoreType.DMA((8,)),
            pltpu.SemaphoreType.DMA((8,)),
            pltpu.SemaphoreType.DMA((8,)),
        ],
        compiler_params=pltpu.CompilerParams(
            collective_id=0, has_side_effects=True, vmem_limit_bytes=56 * 1024 * 1024
        ),
        name="window_block",
    )(raw, jnp.transpose(surface_mask, (1, 0, 2)), logit_scale, mask_bias, w_qkv, w_out, w_up, w_down)

    joined = pl.pallas_call(
        hand_over,
        out_shape=jax.ShapeDtypeStruct(raw.shape, BF16),
        in_specs=[vmem],
        out_specs=anywhere,
        scratch_shapes=[pltpu.SemaphoreType.DMA((groups,))],
        name="hand_over",
    )(pltpu.with_memory_space_constraint(joined, pltpu.VMEM))
    joined = joined.reshape(groups, nlat, nlon, tiles, levels, 128)
    return jnp.transpose(joined, (0, 4, 1, 2, 3, 5)).reshape(fields.shape)


def solution(mesh):
    return jax.shard_map(
        per_device,
        mesh=mesh,
        in_specs=(
            P("grp", None, "lat", "lon", None),
            P(None, "lat", "lon"),
            P(),
            P(),
            P(),
            P(),
            P(),
            P(),
        ),
        out_specs=P("grp", None, "lat", "lon", None),
        check_vma=False,
    )
```

time: 44.8 us -> 40.7 us (0.908)
  Pallas kernels: 44.6 us -> 40.5 us
    pallas_call x1, Pallas kernels: 42.7 us -> 39.6 us  [per_device(): pl.pallas_call(functools.partial(kernel, real, heads), out_shape=pltpu.VM...]
    pallas_call x1, Pallas kernels: 1.92 us -> 0.94 us  [per_device(): pl.pallas_call(hand_over, out_shape=jax.ShapeDtypeStruct(raw.shape, BF16)...]
where the time goes in v1:
time: 40.7 us; the launch traced here: 40.5 us
  Pallas kernels  40.5 us (100%)
    pallas_call x1, Pallas kernels, per_device(): pl.pallas_call(functools.partial(kernel, real, heads), out_shape=pltpu.VM...  39.6 us
    pallas_call x1, Pallas kernels, per_device(): pl.pallas_call(hand_over, out_shape=jax.ShapeDtypeStruct(raw.shape, BF16)...  0.94 us

profile of v1, /device:TPU:1, one launch (start us, length us, event | category | flops | bytes accessed | tf_op | source)
XLA Modules:
  0.0 40.5 jit_solution(5100764044242350971)
XLA Ops:
  0.0 39.6 %window_block.1.src = bf16[3,12,6,16,128]{4,3,2,1,0:T(8,128)(2,1)S(1)} custom-call(bf16[3,12,6,16,128]{4,3,2,1,0:T(8,128)(2,1)} %bitcast.11, s32[12,2,12]{2,1,0:T(2,128)} %bitcast.12, f32[8]{0:T(128)} %scale_hbm.1, f32[8]{0:T(128)} %bias_hbm.1, bf16[512,1536]{1,0:T(8,128)(2,1)} %wqkv_hbm.1, bf16[512,512]{1,0:T(8,128)(2,1)} %wout_hbm.1, ...), custom_call_target="tpu_custom_call" | custom-call | tf_op jit(solution)/shard_map/window_block/pallas_call | solution.py:443
  39.6 0.9 %hand_over.1 = bf16[3,12,6,16,128]{4,3,2,1,0:T(8,128)(2,1)} custom-call(bf16[3,12,6,16,128]{4,3,2,1,0:T(8,128)(2,1)S(1)} %window_block.1.src), custom_call_target="tpu_custom_call" | custom-call | tf_op jit(solution)/shard_map/hand_over/pallas_call | solution.py:488

commit v2 on v1

--- a/solution.py
+++ b/solution.py
@@ -73,6 +73,12 @@
                 pl.semaphore_signal(barrier, inc=1, device_id=peer(d, da, db), device_id_type=MESH)
                 greeted += 1
 
+    last = jnp.where(a == na - 1, mine, 0)
+
+    def slot(d, cc, rr, crossed):
+        same = 1 - (1 - d) * crossed
+        return 4 * d + 2 * (rr + same * (cc - rr)) + cc + same * (rr - cc)
+
     def row_of(parity, rr):
         return (1 + 2 * parity + rr) % 4
 
@@ -92,29 +98,32 @@
                 pl.when(mine == 0)(local)
 
     def stay(cc, rr):
-        i = 2 * rr + cc
+        i = slot(0, cc, rr, 0)
         return pltpu.make_async_copy(block_of(fields_hbm, mine, cc, rr), rin.at[i], recv1.at[i])
 
     def forward(d, cc, rr):
-        i = 4 * d + 2 * rr + cc
+        n = 4 * d + 2 * cc + rr
         parity = (g + b + d + cc) % 2
+        i = slot(d, cc, rr, jnp.where((a - rr * parity + na) % na == na - 1, parity, 0))
         return pltpu.make_async_remote_copy(
             src_ref=block_of(raw, parity, cc, rr), dst_ref=rin.at[i],
-            send_sem=send1.at[i], recv_sem=recv1.at[i],
+            send_sem=send1.at[n], recv_sem=recv1.at[i],
             device_id=peer(d, -rr * parity, -cc), device_id_type=MESH,
         )
 
     def backward(d, cc, rr):
-        i = 4 * d + 2 * rr + cc
+        n = 4 * d + 2 * cc + rr
         return pltpu.make_async_remote_copy(
-            src_ref=rout.at[i], dst_ref=block_of(out_ref, mine, cc, rr),
-            send_sem=send2.at[i], recv_sem=recv2.at[i],
+            src_ref=rout.at[slot(d, cc, rr, last)], dst_ref=block_of(out_ref, mine, cc, rr),
+            send_sem=send2.at[n], recv_sem=recv2.at[n],
             device_id=peer(d, rr * mine, cc), device_id_type=MESH,
         )
 
     def settle(cc, rr):
-        i = 2 * rr + cc
-        return pltpu.make_async_copy(rout.at[i], block_of(out_ref, mine, cc, rr), recv2.at[i])
+        n = 2 * cc + rr
+        return pltpu.make_async_copy(
+            rout.at[slot(0, cc, rr, last)], block_of(out_ref, mine, cc, rr), recv2.at[n]
+        )
 
     def share(n):
         da, db = ((0, -1), (-1, 0), (-1, -1))[n]
@@ -141,8 +150,6 @@
             ((wqkv_hbm, wqkv), (wout_hbm, wout), (wup_hbm, wup), (wdown_hbm, wdown))
         )
     ]
-    for copy in weights:
-        copy.start()
 
     for copy in small:
         copy.wait()
@@ -151,12 +158,15 @@
         tidy[levels * i : levels * (i + 1), : mask_ref.shape[2]] = mask_ref[i].astype(F32)
 
     load.wait()
+    for copy in weights:
+        copy.start()
     pl.semaphore_wait(barrier, greeted)
-    order = [(d, cc, rr) for rr in (0, 1) for cc in (0, 1) for d in (1, 0)]
+    for n in range(3):
+        share(n).start()
+    order = [(0, cc, rr) for rr in (0, 1) for cc in (1, 0)]
+    order += [(1, cc, rr) for cc in (0, 1) for rr in (0, 1)]
     for d, cc, rr in order:
         by_owner(d, cc, rr, None, lambda: forward(d, cc, rr).start())
-    for n in range(3):
-        share(n).start()
 
     def shuffle(count, held, out_rows, raw_out):
         shape = (out_rows, held * tiles) if raw_out else (held * tiles, out_rows)
@@ -173,7 +183,6 @@
         pick[...] = shuffle(count, held, n, False)
         put[...] = shuffle(count, held, n, True)
 
-    last = jnp.where(a == na - 1, mine, 0)
     row_in_block = iota((pair_rows, lanes), 0) % rows
     valid = row_in_block < real
     raw_bias = jnp.zeros((1, lanes), F32)
@@ -195,18 +204,18 @@
     ones = jnp.where(valid, 1.0, 0.0).astype(BF16)
 
     def arrive(p):
-        for cc in (0, 1):
-            i = 2 * p + cc
+        for rr in (0, 1):
+            i = 2 * p + rr
             pltpu.make_async_copy(rin.at[i], rin.at[i], recv1.at[i]).wait()
-        both = jnp.concatenate([rin[2 * p + cc].reshape(slab_rows, 128) for cc in (0, 1)], 1)
+        both = jnp.concatenate([rin[2 * p + rr].reshape(slab_rows, 128) for rr in (0, 1)], 1)
         start = 0
         for (token, _, held, n), pick in zip(cuts, sorts):
             tall = dot(pick[...], both[start : start + n]).astype(BF16)
             start += n
-            for cc in (0, 1):
+            for rr in (0, 1):
                 for t in range(tiles):
-                    win[p, cc, token : token + held, 128 * t : 128 * (t + 1)] = tall[
-                        t * held : (t + 1) * held, 128 * cc : 128 * (cc + 1)
+                    win[p, rr, token : token + held, 128 * t : 128 * (t + 1)] = tall[
+                        t * held : (t + 1) * held, 128 * rr : 128 * (rr + 1)
                     ]
 
     def mark(rr, carry):
@@ -229,7 +238,7 @@
             marks = dot(by_cell, jnp.ones((128, lanes), BF16))
             key = (marks * bias_row + far).astype(BF16)
             for d in (0, 1):
-                at = pl.multiple_of((2 * d + rr) * pair_rows + cc * rows, 16)
+                at = pl.multiple_of(slot(d, cc, rr, last) * rows, 16)
                 kx[pl.ds(at, rows)] = key
         return carry
 
@@ -273,12 +282,13 @@
 
     q_lane = iota((pair_rows, lanes), 1)
     low = q_lane < head_size
+    lower = jnp.where(iota((pair_rows, lanes), 0) >= rows, 1, 0)
     sides = [jnp.where(low if e == 0 else ~low, 1.0, 0.0).astype(BF16) for e in (0, 1)]
     ones_all = jnp.concatenate([ones, ones], 0)
 
     def attend(q, k0, sink):
         here = pl.ds(pl.multiple_of(q * pair_rows, 16), pair_rows)
-        q_late = (q % 2 * last).astype(F32)
+        q_late = (last * (q % 2 + q // 2 * (lower - q % 2))).astype(F32)
         q_region = jnp.where(
             q_lane == 2 * heads, 1 - q_late, jnp.where(q_lane == 2 * heads + 1, q_late, 0.0)
         )
@@ -357,32 +367,37 @@
                 [
                     jnp.concatenate(
                         [
-                            joined[cc * rows + token : cc * rows + token + held, 128 * t : 128 * (t + 1)]
+                            joined[rr * rows + token : rr * rows + token + held, 128 * t : 128 * (t + 1)]
                             for t in range(tiles)
                         ],
                         0,
                     )
-                    for cc in (0, 1)
+                    for rr in (0, 1)
                 ],
                 1,
             )
             flat.append(dot(put[...], tall).astype(BF16))
         flat = jnp.concatenate(flat, 0)
-        d, rr = p // 2, p % 2
-        for cc in (1, 0):
-            rout[2 * p + cc] = flat[:, 128 * cc : 128 * (cc + 1)].reshape(slab)
-            if cc == 1:
-                backward(d, cc, rr).start()
-            else:
-                away = d + rr * mine
-                pl.when(away > 0)(lambda: backward(d, 0, rr).start())
-                pl.when(away == 0)(lambda: settle(0, rr).start())
+        d, other = p // 2, p % 2
+        for k in (1, 0):
+            rout[2 * p + k] = flat[:, 128 * k : 128 * (k + 1)].reshape(slab)
+            same = 1 - (1 - d) * last
+            cc, rr = k + same * (other - k), other + same * (k - other)
+            away = d + cc + rr * mine
+            pl.when(away > 0)(lambda: backward(d, cc, rr).start())
+            pl.when(away == 0)(lambda: settle(cc, rr).start())
 
     weights[0].wait()
+
+    def mark_all():
+        for n in range(3):
+            pltpu.make_async_copy(marked.at[n], marked.at[n], mrecv.at[n]).wait()
+        lax.fori_loop(0, 2, mark, 0)
 
     def gather(t, carry):
         arrive(t)
         project(t)
+        pl.when(t == 1)(mark_all)
         first = jnp.where(t == 1, 0, t)
         lax.fori_loop(first, jnp.where(t == 0, 0, t + 1), attend_near, 0)
         return carry
@@ -393,9 +408,6 @@
         join(p)
         return carry
 
-    for n in range(3):
-        pltpu.make_async_copy(marked.at[n], marked.at[n], mrecv.at[n]).wait()
-    lax.fori_loop(0, 2, mark, 0)
     lax.fori_loop(0, 4, gather, 0)
     for copy in weights[1:]:
         copy.wait()
@@ -409,7 +421,7 @@
         by_owner(d, cc, rr, None, lambda: backward(d, cc, rr).wait_send())
     for d, cc, rr in order:
         landed = block_of(out_ref, (g + b + d + cc) % 2, cc, rr)
-        pltpu.make_async_copy(landed, landed, recv2.at[4 * d + 2 * rr + cc]).wait()
+        pltpu.make_async_copy(landed, landed, recv2.at[4 * d + 2 * cc + rr]).wait()
 
 
 def hand_over(src, dst, sem):

time: 40.7 us -> 37.1 us (0.912)
  Pallas kernels: 40.5 us -> 36.9 us
    pallas_call x1, Pallas kernels: 39.6 us -> 35.9 us  [per_device(): pl.pallas_call(functools.partial(kernel, real, heads), out_shape=pltpu.VM...]
where the time goes in v2:
time: 37.1 us; the launch traced here: 36.9 us
  Pallas kernels  36.9 us (99%)
    pallas_call x1, Pallas kernels, per_device(): pl.pallas_call(functools.partial(kernel, real, heads), out_shape=pltpu.VM...  35.9 us
    pallas_call x1, Pallas kernels, per_device(): pl.pallas_call(hand_over, out_shape=jax.ShapeDtypeStruct(raw.shape, BF16)...  0.94 us

profile of v2, /device:TPU:1, one launch (start us, length us, event | category | flops | bytes accessed | tf_op | source)
XLA Modules:
  0.0 36.9 jit_solution(2683587060812530157)
XLA Ops:
  0.0 35.9 %window_block.1.src = bf16[3,12,6,16,128]{4,3,2,1,0:T(8,128)(2,1)S(1)} custom-call(bf16[3,12,6,16,128]{4,3,2,1,0:T(8,128)(2,1)} %bitcast.11, s32[12,2,12]{2,1,0:T(2,128)} %bitcast.12, f32[8]{0:T(128)} %scale_hbm.1, f32[8]{0:T(128)} %bias_hbm.1, bf16[512,1536]{1,0:T(8,128)(2,1)} %wqkv_hbm.1, bf16[512,512]{1,0:T(8,128)(2,1)} %wout_hbm.1, ...), custom_call_target="tpu_custom_call" | custom-call | tf_op jit(solution)/shard_map/window_block/pallas_call | solution.py:455
  36.0 0.9 %hand_over.1 = bf16[3,12,6,16,128]{4,3,2,1,0:T(8,128)(2,1)} custom-call(bf16[3,12,6,16,128]{4,3,2,1,0:T(8,128)(2,1)S(1)} %window_block.1.src), custom_call_target="tpu_custom_call" | custom-call | tf_op jit(solution)/shard_map/hand_over/pallas_call | solution.py:500

commit v3 on v2

--- a/solution.py
+++ b/solution.py
@@ -76,7 +76,7 @@
     last = jnp.where(a == na - 1, mine, 0)
 
     def slot(d, cc, rr, crossed):
-        same = 1 - (1 - d) * crossed
+        same = 1 - crossed
         return 4 * d + 2 * (rr + same * (cc - rr)) + cc + same * (rr - cc)
 
     def row_of(parity, rr):
@@ -282,13 +282,12 @@
 
     q_lane = iota((pair_rows, lanes), 1)
     low = q_lane < head_size
-    lower = jnp.where(iota((pair_rows, lanes), 0) >= rows, 1, 0)
     sides = [jnp.where(low if e == 0 else ~low, 1.0, 0.0).astype(BF16) for e in (0, 1)]
     ones_all = jnp.concatenate([ones, ones], 0)
 
     def attend(q, k0, sink):
         here = pl.ds(pl.multiple_of(q * pair_rows, 16), pair_rows)
-        q_late = (last * (q % 2 + q // 2 * (lower - q % 2))).astype(F32)
+        q_late = (last * (q % 2)).astype(F32)
         q_region = jnp.where(
             q_lane == 2 * heads, 1 - q_late, jnp.where(q_lane == 2 * heads + 1, q_late, 0.0)
         )
@@ -381,7 +380,7 @@
         d, other = p // 2, p % 2
         for k in (1, 0):
             rout[2 * p + k] = flat[:, 128 * k : 128 * (k + 1)].reshape(slab)
-            same = 1 - (1 - d) * last
+            same = 1 - last
             cc, rr = k + same * (other - k), other + same * (k - other)
             away = d + cc + rr * mine
             pl.when(away > 0)(lambda: backward(d, cc, rr).start())
@@ -403,7 +402,7 @@
         return carry
 
     def scatter(t, carry):
-        p = 3 - t
+        p = jnp.where(t == 1, 2 - last, jnp.where(t == 2, 1 + last, 3 - t))
         attend_far(p)
         join(p)
         return carry

time: 37.1 us -> 35.4 us (0.954)
  Pallas kernels: 36.9 us -> 35.2 us
    pallas_call x1, Pallas kernels: 35.9 us -> 34.2 us  [per_device(): pl.pallas_call(functools.partial(kernel, real, heads), out_shape=pltpu.VM...]
where the time goes in v3:
time: 35.4 us; the launch traced here: 35.2 us
  Pallas kernels  35.2 us (99%)
    pallas_call x1, Pallas kernels, per_device(): pl.pallas_call(functools.partial(kernel, real, heads), out_shape=pltpu.VM...  34.2 us
    pallas_call x1, Pallas kernels, per_device(): pl.pallas_call(hand_over, out_shape=jax.ShapeDtypeStruct(raw.shape, BF16)...  0.94 us

profile of v3, /device:TPU:1, one launch (start us, length us, event | category | flops | bytes accessed | tf_op | source)
XLA Modules:
  0.0 35.2 jit_solution(12497301446758877478)
XLA Ops:
  0.0 34.2 %window_block.1.src = bf16[3,12,6,16,128]{4,3,2,1,0:T(8,128)(2,1)S(1)} custom-call(bf16[3,12,6,16,128]{4,3,2,1,0:T(8,128)(2,1)} %bitcast.11, s32[12,2,12]{2,1,0:T(2,128)} %bitcast.12, f32[8]{0:T(128)} %scale_hbm.1, f32[8]{0:T(128)} %bias_hbm.1, bf16[512,1536]{1,0:T(8,128)(2,1)} %wqkv_hbm.1, bf16[512,512]{1,0:T(8,128)(2,1)} %wout_hbm.1, ...), custom_call_target="tpu_custom_call" | custom-call | tf_op jit(solution)/shard_map/window_block/pallas_call | solution.py:454
  34.2 0.9 %hand_over.1 = bf16[3,12,6,16,128]{4,3,2,1,0:T(8,128)(2,1)} custom-call(bf16[3,12,6,16,128]{4,3,2,1,0:T(8,128)(2,1)S(1)} %window_block.1.src), custom_call_target="tpu_custom_call" | custom-call | tf_op jit(solution)/shard_map/hand_over/pallas_call | solution.py:499

commit v4 on v3

--- a/solution.py
+++ b/solution.py
@@ -163,8 +163,8 @@
     pl.semaphore_wait(barrier, greeted)
     for n in range(3):
         share(n).start()
-    order = [(0, cc, rr) for rr in (0, 1) for cc in (1, 0)]
-    order += [(1, cc, rr) for cc in (0, 1) for rr in (0, 1)]
+    order = [(1, 0, 0), (0, 1, 0), (0, 0, 0), (0, 1, 1), (0, 0, 1)]
+    order += [(1, 0, 1), (1, 1, 0), (1, 1, 1)]
     for d, cc, rr in order:
         by_owner(d, cc, rr, None, lambda: forward(d, cc, rr).start())
 

time: 35.4 us -> 35.5 us (level)
  no operation moved by 1% of the time
where the time goes in v4:
time: 35.5 us; the launch traced here: 35.3 us
  Pallas kernels  35.3 us (99%)
    pallas_call x1, Pallas kernels, per_device(): pl.pallas_call(functools.partial(kernel, real, heads), out_shape=pltpu.VM...  34.3 us
    pallas_call x1, Pallas kernels, per_device(): pl.pallas_call(hand_over, out_shape=jax.ShapeDtypeStruct(raw.shape, BF16)...  0.94 us

profile of v4, /device:TPU:1, one launch (start us, length us, event | category | flops | bytes accessed | tf_op | source)
XLA Modules:
  0.0 35.3 jit_solution(3156718042654132079)
XLA Ops:
  0.0 34.3 %window_block.1.src = bf16[3,12,6,16,128]{4,3,2,1,0:T(8,128)(2,1)S(1)} custom-call(bf16[3,12,6,16,128]{4,3,2,1,0:T(8,128)(2,1)} %bitcast.11, s32[12,2,12]{2,1,0:T(2,128)} %bitcast.12, f32[8]{0:T(128)} %scale_hbm.1, f32[8]{0:T(128)} %bias_hbm.1, bf16[512,1536]{1,0:T(8,128)(2,1)} %wqkv_hbm.1, bf16[512,512]{1,0:T(8,128)(2,1)} %wout_hbm.1, ...), custom_call_target="tpu_custom_call" | custom-call | tf_op jit(solution)/shard_map/window_block/pallas_call | solution.py:454
  34.3 0.9 %hand_over.1 = bf16[3,12,6,16,128]{4,3,2,1,0:T(8,128)(2,1)} custom-call(bf16[3,12,6,16,128]{4,3,2,1,0:T(8,128)(2,1)S(1)} %window_block.1.src), custom_call_target="tpu_custom_call" | custom-call | tf_op jit(solution)/shard_map/hand_over/pallas_call | solution.py:499
